TPU v7x, 32 devices: a whole 2x2x4 slice. The times are simulated.
32 devices in a mesh: wide: 8 (over z, x), group: 4 (over y, core).
Axes of the slice: x: 2, y: 2, z: 4, core: 2. Of those that a mesh axis runs over, the one named last changes fastest.
Arguments:
- feat4: bfloat16 [32, 24, 24, 256], P(('wide', 'group')), may hold values from -100 to 100
- feat5: bfloat16 [32, 12, 12, 256], P(('wide', 'group')), may hold values from -100 to 100
- feat6: bfloat16 [32, 6, 6, 256], P(('wide', 'group')), may hold values from -100 to 100
- feat7: bfloat16 [32, 3, 3, 256], P(('wide', 'group')), may hold values from -100 to 100
- out_grad4: bfloat16 [32, 24, 24, 256], P(('wide', 'group')), may hold values from -6 to 6
- out_grad5: bfloat16 [32, 12, 12, 256], P(('wide', 'group')), may hold values from -6 to 6
- out_grad6: bfloat16 [32, 6, 6, 256], P(('wide', 'group')), may hold values from -6 to 6
- out_grad7: bfloat16 [32, 3, 3, 256], P(('wide', 'group')), may hold values from -6 to 6
- conv_weight: bfloat16 [3, 3, 256, 256], replicated, may hold values from -0.125 to 0.125
- bn_gain: float32 [4, 256], replicated, may hold values from 0.25 to 1.75
- bn_shift: float32 [4, 256], replicated, may hold values from -0.5 to 0.5
- heights: int32 [32], P(('wide', 'group')), may hold values from 168 to 384
- widths: int32 [32], P(('wide', 'group')), may hold values from 168 to 384
Outputs:
- out4: bfloat16 [32, 24, 24, 256], P(('wide', 'group'))
- out5: bfloat16 [32, 12, 12, 256], P(('wide', 'group'))
- out6: bfloat16 [32, 6, 6, 256], P(('wide', 'group'))
- out7: bfloat16 [32, 3, 3, 256], P(('wide', 'group'))
- d_feat4: bfloat16 [32, 24, 24, 256], P(('wide', 'group'))
- d_feat5: bfloat16 [32, 12, 12, 256], P(('wide', 'group'))
- d_feat6: bfloat16 [32, 6, 6, 256], P(('wide', 'group'))
- d_feat7: bfloat16 [32, 3, 3, 256], P(('wide', 'group'))
- d_weight: float32 [3, 3, 256, 256], replicated
- d_gain: float32 [4, 256], replicated
- d_shift: float32 [4, 256], replicated
Inputs may be any that keep to these rules, and one draw needn't show every extreme that they name: `heights`: pixel height of the valid part of each image. `widths`: pixel width of the valid part of each image.
All inputs are finite; a program needn't handle non-finite values.
Results may differ from a plain program's by a relative error of at most 0.0049.
Values sent between devices are 32-bit elements; how exact they have to be, the bound alone decides.
No kernel may reach another device: no remote copies, remote signals or barrier semaphores. Data moves between devices by JAX's collectives and lax.ppermute only.
A program may use at most 64 MiB of HBM per device.

v0:
```python
import jax
import jax.numpy as jnp
from jax import lax
from jax.sharding import PartitionSpec as P

EPSILON = 1e-05


def level_mask(heights, widths, stride, extent):
    row_limit = (heights[0] + stride - 1) // stride
    col_limit = (widths[0] + stride - 1) // stride
    row_place = lax.broadcasted_iota(jnp.int32, (extent, extent), 0)
    col_place = lax.broadcasted_iota(jnp.int32, (extent, extent), 1)
    inside = jnp.logical_and(row_place < row_limit, col_place < col_limit)
    return (inside.astype(jnp.float32), row_limit)


def conv_rows(padded, conv_weight, start_row, row_count, extent):
    summed = jnp.zeros((row_count * extent, conv_weight.shape[3]), jnp.float32)
    for tap_row in range(3):
        for tap_col in range(3):
            window = lax.dynamic_slice_in_dim(padded, start_row + tap_row, row_count, 0)[
                :, tap_col : tap_col + extent, :
            ]
            summed = summed + jnp.dot(
                window.reshape(row_count * extent, -1),
                conv_weight[tap_row, tap_col],
                preferred_element_type=jnp.float32,
            )
    return summed.reshape(row_count, extent, -1)


def input_grad_rows(padded_back, conv_weight, start_row, row_count, extent):
    summed = jnp.zeros((row_count * extent, conv_weight.shape[2]), jnp.float32)
    for tap_row in range(3):
        for tap_col in range(3):
            window = lax.dynamic_slice_in_dim(padded_back, start_row + 2 - tap_row, row_count, 0)[
                :, 2 - tap_col : 2 - tap_col + extent, :
            ]
            summed = summed + lax.dot_general(
                window.reshape(row_count * extent, -1),
                conv_weight[tap_row, tap_col],
                (((1,), (1,)), ((), ())),
                preferred_element_type=jnp.float32,
            )
    return summed.reshape(row_count, extent, -1)


def weight_grad_rows(padded, back_rows, start_row, row_count, extent):
    flat_back = back_rows.reshape(row_count * extent, -1)
    tap_terms = []
    for tap_row in range(3):
        for tap_col in range(3):
            window = lax.dynamic_slice_in_dim(padded, start_row + tap_row, row_count, 0)[
                :, tap_col : tap_col + extent, :
            ]
            tap_terms.append(
                lax.dot_general(
                    window.reshape(row_count * extent, -1),
                    flat_back,
                    (((0,), (0,)), ((), ())),
                    preferred_element_type=jnp.float32,
                )
            )
    return jnp.stack(tap_terms).reshape(3, 3, padded.shape[2], flat_back.shape[1])


def forward_conv(padded, conv_weight, extent):
    conv_out = conv_rows(padded, conv_weight, 0, extent, extent)
    return conv_out


def backward_conv(padded, back_grad, conv_weight, extent):
    padded_back = jnp.pad(back_grad, ((1, 1), (1, 1), (0, 0)))
    weight_part = weight_grad_rows(padded, back_grad, 0, extent, extent)
    input_part = input_grad_rows(padded_back, conv_weight, 0, extent, extent)
    return (weight_part, input_part)


def combine_stats(values):
    within = lax.psum(values, "group")
    result = lax.psum(within, "wide")
    return result


def combine_grads(values):
    within = lax.psum(values, "group")
    result = lax.psum(within, "wide")
    return result


def shards(
    feat4,
    feat5,
    feat6,
    feat7,
    out_grad4,
    out_grad5,
    out_grad6,
    out_grad7,
    conv_weight,
    bn_gain,
    bn_shift,
    heights,
    widths,
):
    features = (feat4, feat5, feat6, feat7)
    cotangents = (out_grad4, out_grad5, out_grad6, out_grad7)
    devices = lax.axis_size("wide") * lax.axis_size("group")
    levels = []
    for level_index in range(4):
        feature = features[level_index][0]
        extent = feature.shape[0]
        valid_mask, row_limit = level_mask(heights, widths, 16 * 2**level_index, extent)
        weighted = valid_mask[:, :, None]
        padded = jnp.pad(feature * weighted.astype(feature.dtype), ((1, 1), (1, 1), (0, 0)))
        conv_out = forward_conv(padded, conv_weight, extent)
        levels.append((valid_mask, row_limit, weighted, padded, conv_out))
    moments = []
    local_sums = jnp.stack(
        [jnp.sum(level_entry[4] * level_entry[2], axis=(0, 1)) for level_entry in levels]
    )
    local_squares = jnp.stack(
        [
            jnp.sum(level_entry[2] * level_entry[4] * level_entry[4], axis=(0, 1))
            for level_entry in levels
        ]
    )
    local_counts = jnp.stack([jnp.sum(level_entry[0]) for level_entry in levels])
    moment_sums, squares, counts = combine_stats((local_sums, local_squares, local_counts))
    for level_index in range(4):
        pixel_count = counts[level_index]
        mean_value = moment_sums[level_index] / pixel_count
        moments.append(
            (pixel_count, mean_value, squares[level_index] / pixel_count - mean_value * mean_value)
        )
    finals = []
    for level_index in range(4):
        valid_mask, row_limit, weighted, padded, conv_out = levels[level_index]
        pixel_count, mean_value, variance = moments[level_index]
        inverse = lax.rsqrt(variance + EPSILON)
        normed = (conv_out - mean_value) * inverse
        shifted = bn_gain[level_index] * normed + bn_shift[level_index]
        sigmoid_value = jax.nn.sigmoid(shifted)
        output = (weighted * shifted * sigmoid_value).astype(jnp.bfloat16)
        slope_term = (
            weighted
            * cotangents[level_index][0].astype(jnp.float32)
            * sigmoid_value
            * (1.0 + shifted * (1.0 - sigmoid_value))
        )
        finals.append((output, normed, inverse, slope_term))
    shift_local = jnp.stack([jnp.sum(final_entry[3], axis=(0, 1)) for final_entry in finals])
    gain_local = jnp.stack(
        [jnp.sum(final_entry[3] * final_entry[1], axis=(0, 1)) for final_entry in finals]
    )
    shift_rows, gain_rows = combine_stats((shift_local, gain_local))
    back_sums = [(shift_rows[level_index], gain_rows[level_index]) for level_index in range(4)]
    weight_local = jnp.zeros(conv_weight.shape, jnp.float32)
    outputs = []
    input_grads = []
    shift_list = []
    gain_list = []
    for level_index in range(4):
        valid_mask, row_limit, weighted, padded, conv_out = levels[level_index]
        pixel_count, mean_value, variance = moments[level_index]
        output, normed, inverse, slope_term = finals[level_index]
        shift_sum, gain_sum = back_sums[level_index]
        extent = conv_out.shape[0]
        back_grad = (
            weighted
            * (bn_gain[level_index] * inverse)
            * (slope_term - shift_sum / pixel_count - normed * (gain_sum / pixel_count))
        ).astype(jnp.bfloat16)
        weight_part, input_part = backward_conv(padded, back_grad, conv_weight, extent)
        weight_local = weight_local + weight_part
        input_grads.append((weighted * input_part).astype(jnp.bfloat16)[None])
        outputs.append(output[None])
        shift_list.append(shift_sum)
        gain_list.append(gain_sum)
    weight_total = combine_grads(weight_local)
    return (
        outputs[0],
        outputs[1],
        outputs[2],
        outputs[3],
        input_grads[0],
        input_grads[1],
        input_grads[2],
        input_grads[3],
        weight_total / devices,
        jnp.stack(gain_list) / devices,
        jnp.stack(shift_list) / devices,
    )


def solution(mesh):
    placed = (
        P(("wide", "group"), None, None, None),
        P(("wide", "group"), None, None, None),
        P(("wide", "group"), None, None, None),
        P(("wide", "group"), None, None, None),
        P(("wide", "group"), None, None, None),
        P(("wide", "group"), None, None, None),
        P(("wide", "group"), None, None, None),
        P(("wide", "group"), None, None, None),
        P(),
        P(),
        P(),
        P(("wide", "group")),
        P(("wide", "group")),
    )
    return jax.shard_map(
        shards,
        mesh=mesh,
        in_specs=placed,
        out_specs=(
            P(("wide", "group"), None, None, None),
            P(("wide", "group"), None, None, None),
            P(("wide", "group"), None, None, None),
            P(("wide", "group"), None, None, None),
            P(("wide", "group"), None, None, None),
            P(("wide", "group"), None, None, None),
            P(("wide", "group"), None, None, None),
            P(("wide", "group"), None, None, None),
            P(),
            P(),
            P(),
        ),
        check_vma=False,
    )
```

profile of v0, /device:TPU:0, one launch (start us, length us, event | category | flops | bytes accessed | tf_op | source)
XLA Modules:
  0.0 299.1 jit_solution(16657673691624110499)
XLA Ops:
  17.4 1.0 fusion.131
  18.4 1.1 convolution_add_fusion.63
  19.4 1.1 convolution_add_fusion.62
  35.5 2.6 pad_maximum_fusion.4
  38.2 8.7 %all-reduce.11 = (f32[4,256]{1,0:T(4,128)S(1)}, f32[4]{0:T(128)S(1)}, f32[4,256]{1,0:T(4,128)S(1)}) all-reduce(f32[4,256]{1,0:T(4,128)S(1)} %pad_maximum_fusion.1, f32[4]{0:T(128)S(1)} %pad_maximum_fusion.4, f32[4,256]{1,0:T(4,128)S(1)} %pad_maximum_fusion), channel_id=1, replica_groups=mesh['wide'=8,'group'=4] {'group'}, use_global_device_ids=true, to_apply=%region_16.17 | all-reduce | flops 2052 | bytes 16416 | tf_op jit(solution)/shard_map/psum | solution.py:81
  46.9 22.2 %all-reduce.9 = (f32[4,256]{1,0:T(4,128)S(1)}, f32[4]{0:T(128)S(1)}, f32[4,256]{1,0:T(4,128)S(1)}) all-reduce(f32[4,256]{1,0:T(4,128)S(1)} %get-tuple-element.34, f32[4]{0:T(128)S(1)} %get-tuple-element.35, f32[4,256]{1,0:T(4,128)S(1)} %get-tuple-element.36), channel_id=1, replica_groups=mesh['wide'=8,'group'=4] {'wide'}, use_global_device_ids=true, to_apply=%region_17.18 | all-reduce | flops 2052 | bytes 16416 | tf_op jit(solution)/shard_map/psum | solution.py:82
  69.7 2.6 slice_divide_fusion.8
  72.3 2.6 slice_divide_fusion.9
  78.9 5.9 %all-reduce.10 = (f32[4,256]{1,0:T(4,128)S(1)}, f32[4,256]{1,0:T(4,128)S(1)}) all-reduce(f32[4,256]{1,0:T(4,128)S(1)} %pad_maximum_fusion.3, f32[4,256]{1,0:T(4,128)S(1)} %pad_maximum_fusion.2), channel_id=1, replica_groups=mesh['wide'=8,'group'=4] {'group'}, use_global_device_ids=true, to_apply=%region_28.29 | all-reduce | flops 2048 | bytes 16384 | tf_op jit(solution)/shard_map/psum | solution.py:81
  84.8 17.6 %all-reduce.8 = (f32[4,256]{1,0:T(4,128)S(1)}, f32[4,256]{1,0:T(4,128)S(1)}) all-reduce(f32[4,256]{1,0:T(4,128)S(1)} %get-tuple-element.32, f32[4,256]{1,0:T(4,128)S(1)} %get-tuple-element.33), channel_id=1, replica_groups=mesh['wide'=8,'group'=4] {'wide'}, use_global_device_ids=true, to_apply=%region_29.30 | all-reduce | flops 2048 | bytes 16384 | tf_op jit(solution)/shard_map/psum | solution.py:82
  102.4 2.6 slice_divide_fusion
  105.1 2.6 slice_divide_fusion.1
  107.9 1.1 multiply_convert_fusion.2
  120.9 2.1 add_add_fusion
  127.0 1.3 reshape.1156
  128.3 1.3 reshape.1150
  129.6 1.3 reshape.1151
  130.9 1.3 reshape.1152
  132.2 1.3 reshape.1153
  135.9 0.9 convolution_add_fusion.54
  137.6 1.0 convolution_add_fusion.52
  140.1 1.4 multiply_convert_fusion.21
  145.3 0.9 convolution_add_fusion.39
  146.2 0.9 convolution_add_fusion.38
  147.1 0.9 convolution_add_fusion.37
  148.1 1.0 convolution_add_fusion.36
  153.2 1.2 pad_slice_fusion
  156.1 20.6 %all-reduce.15.cloned.1.call-done = f32[3,3,256,256]{3,2,1,0:T(8,128)} async-done(((f32[3,3,256,256]{3,2,1,0:T(8,128)}), f32[3,3,256,256]{3,2,1,0:T(8,128)}) %all-reduce.15.cloned.1.call-update) | async-done | bytes 2359312 | tf_op jit(solution)/shard_map/psum | solution.py:87
  176.7 1.9 multiply_convert_fusion.6
  181.7 1.1 multiply_convert_fusion.1
  182.7 106.2 %all-reduce.17.cloned.1.call-done = f32[3,3,256,256]{3,2,1,0:T(8,128)} async-done(((f32[3,3,256,256]{3,2,1,0:T(8,128)}), f32[3,3,256,256]{3,2,1,0:T(8,128)}) %all-reduce.17.cloned.1.call-update) | async-done | bytes 2359312 | tf_op jit(solution)/shard_map/psum | solution.py:88
  289.0 3.3 %broadcast_multiply_fusion = f32[3,3,256,256]{3,2,1,0:T(8,128)} fusion(f32[3,3,256,256]{3,2,1,0:T(8,128)} %all-reduce.17.cloned.1.call-done), kind=kLoop, calls=%fused_computation.17 | loop fusion | flops 589824 | bytes 4718592 | tf_op jit(solution)/shard_map/div | solution.py:191
  (492 shorter events, 59.5 us)
Async XLA Ops:
  7.2 16.6 %copy-start.9 = (bf16[1,12,12,256]{3,2,1,0:T(8,128)(2,1)S(1)}, bf16[1,12,12,256]{3,2,1,0:T(8,128)(2,1)}, u32[]{:S(2)}) copy-start(bf16[1,12,12,256]{3,2,1,0:T(8,128)(2,1)} %param.14) | copy-start | bytes 221188
  7.2 169.5 %all-reduce.15.cloned.1.call-start = ((), (), s32[]{:S(2)}) async-start(), calls=%async_computation | async-start | bytes 4718592 | tf_op jit(solution)/shard_map/psum | solution.py:87
  32.2 45.2 %copy-start.45 = (f32[1,256]{1,0:T(1,128)}, f32[1,256]{1,0:T(1,128)S(1)}, u32[]{:S(2)}) copy-start(f32[1,256]{1,0:T(1,128)S(1)} %get-tuple-element.118) | copy-start | bytes 3076
  32.2 45.6 %copy-start.66 = (f32[1,256]{1,0:T(1,128)}, f32[1,256]{1,0:T(1,128)S(1)}, u32[]{:S(2)}) copy-start(f32[1,256]{1,0:T(1,128)S(1)} %get-tuple-element.117) | copy-start | bytes 3076
  32.2 45.7 %copy-start.69 = (f32[1,256]{1,0:T(1,128)}, f32[1,256]{1,0:T(1,128)S(1)}, u32[]{:S(2)}) copy-start(f32[1,256]{1,0:T(1,128)S(1)} %get-tuple-element.119) | copy-start | bytes 3076
  32.2 45.9 %copy-start.98 = (f32[1,256]{1,0:T(1,128)}, f32[1,256]{1,0:T(1,128)S(1)}, u32[]{:S(2)}) copy-start(f32[1,256]{1,0:T(1,128)S(1)} %get-tuple-element.116) | copy-start | bytes 3076
  32.3 45.1 %copy-start.56 = (f32[1,256]{1,0:T(1,128)}, f32[1,256]{1,0:T(1,128)S(1)}, u32[]{:S(2)}) copy-start(f32[1,256]{1,0:T(1,128)S(1)} %get-tuple-element.130) | copy-start | bytes 3076
  32.3 45.5 %copy-start.84 = (f32[1,256]{1,0:T(1,128)}, f32[1,256]{1,0:T(1,128)S(1)}, u32[]{:S(2)}) copy-start(f32[1,256]{1,0:T(1,128)S(1)} %get-tuple-element.129) | copy-start | bytes 3076
  32.3 45.7 %copy-start.87 = (f32[1,256]{1,0:T(1,128)}, f32[1,256]{1,0:T(1,128)S(1)}, u32[]{:S(2)}) copy-start(f32[1,256]{1,0:T(1,128)S(1)} %get-tuple-element.131) | copy-start | bytes 3076
  32.3 45.8 %copy-start.100 = (f32[1,256]{1,0:T(1,128)}, f32[1,256]{1,0:T(1,128)S(1)}, u32[]{:S(2)}) copy-start(f32[1,256]{1,0:T(1,128)S(1)} %get-tuple-element.128) | copy-start | bytes 3076
  34.6 42.8 %copy-start.1 = (bf16[1,24,24,256]{3,2,1,0:T(8,128)(2,1)S(1)}, bf16[1,24,24,256]{3,2,1,0:T(8,128)(2,1)}, u32[]{:S(2)}) copy-start(bf16[1,24,24,256]{3,2,1,0:T(8,128)(2,1)} %param.17) | copy-start | bytes 884740
  34.6 42.8 %copy-start.18 = (f32[24,24]{1,0:T(8,128)S(1)}, f32[24,24]{1,0:T(8,128)}, u32[]{:S(2)}) copy-start(f32[24,24]{1,0:T(8,128)} %get-tuple-element.150) | copy-start | bytes 6916
  35.2 42.6 %copy-start.7 = (bf16[1,12,12,256]{3,2,1,0:T(8,128)(2,1)S(1)}, bf16[1,12,12,256]{3,2,1,0:T(8,128)(2,1)}, u32[]{:S(2)}) copy-start(bf16[1,12,12,256]{3,2,1,0:T(8,128)(2,1)} %param.18) | copy-start | bytes 221188
  35.2 42.8 %copy-start.16 = (bf16[1,6,6,256]{3,2,1,0:T(8,128)(2,1)S(1)}, bf16[1,6,6,256]{3,2,1,0:T(8,128)(2,1)}, u32[]{:S(2)}) copy-start(bf16[1,6,6,256]{3,2,1,0:T(8,128)(2,1)} %param.19) | copy-start | bytes 55300
  35.2 42.8 %copy-start.37 = (f32[6,6]{1,0:T(8,128)S(1)}, f32[6,6]{1,0:T(8,128)}, u32[]{:S(2)}) copy-start(f32[6,6]{1,0:T(8,128)} %get-tuple-element.146) | copy-start | bytes 436
  35.2 43.0 %copy-start.26 = (f32[3,3,256]{2,1,0:T(4,128)S(1)}, f32[3,3,256]{2,1,0:T(4,128)}, u32[]{:S(2)}) copy-start(f32[3,3,256]{2,1,0:T(4,128)} %reshape.1121) | copy-start | bytes 27652
  35.2 43.0 %copy-start.48 = (f32[3,3]{1,0:T(4,128)S(1)}, f32[3,3]{1,0:T(4,128)}, u32[]{:S(2)}) copy-start(f32[3,3]{1,0:T(4,128)} %get-tuple-element.144) | copy-start | bytes 112
  35.2 43.0 %copy-start.74 = (bf16[1,3,3,256]{3,2,1,0:T(4,128)(2,1)S(1)}, bf16[1,3,3,256]{3,2,1,0:T(4,128)(2,1)}, u32[]{:S(2)}) copy-start(bf16[1,3,3,256]{3,2,1,0:T(4,128)(2,1)} %param.20) | copy-start | bytes 13828
  75.0 32.8 %copy-start.42 = (f32[1,256]{1,0:T(1,128)}, f32[1,256]{1,0:T(1,128)S(1)}, u32[]{:S(2)}) copy-start(f32[1,256]{1,0:T(1,128)S(1)} %get-tuple-element.123) | copy-start | bytes 3076
  75.0 32.8 %copy-start.60 = (f32[1,256]{1,0:T(1,128)}, f32[1,256]{1,0:T(1,128)S(1)}, u32[]{:S(2)}) copy-start(f32[1,256]{1,0:T(1,128)S(1)} %get-tuple-element.122) | copy-start | bytes 3076
  75.0 32.8 %copy-start.63 = (f32[1,256]{1,0:T(1,128)}, f32[1,256]{1,0:T(1,128)S(1)}, u32[]{:S(2)}) copy-start(f32[1,256]{1,0:T(1,128)S(1)} %get-tuple-element.121) | copy-start | bytes 3076
  75.0 32.8 %copy-start.72 = (f32[1,256]{1,0:T(1,128)}, f32[1,256]{1,0:T(1,128)S(1)}, u32[]{:S(2)}) copy-start(f32[1,256]{1,0:T(1,128)S(1)} %get-tuple-element.120) | copy-start | bytes 3076
  75.6 32.2 %copy-start.81 = (f32[256]{0:T(256)}, f32[256]{0:T(256)S(1)}, u32[]{:S(2)}) copy-start(f32[256]{0:T(256)S(1)} %get-tuple-element.137) | copy-start | bytes 3076
  76.2 31.6 %copy-start.92 = (f32[256]{0:T(256)}, f32[256]{0:T(256)S(1)}, u32[]{:S(2)}) copy-start(f32[256]{0:T(256)S(1)} %get-tuple-element.135) | copy-start | bytes 3076
  76.8 31.1 %copy-start.78 = (f32[256]{0:T(256)}, f32[256]{0:T(256)S(1)}, u32[]{:S(2)}) copy-start(f32[256]{0:T(256)S(1)} %get-tuple-element.139) | copy-start | bytes 3076
  77.4 30.5 %copy-start.52 = (f32[256]{0:T(256)}, f32[256]{0:T(256)S(1)}, u32[]{:S(2)}) copy-start(f32[256]{0:T(256)S(1)} %get-tuple-element.141) | copy-start | bytes 3076
  105.1 14.1 %copy-start.111 = (f32[1,256]{1,0:T(1,128)}, f32[1,256]{1,0:T(1,128)S(1)}, u32[]{:S(2)}) copy-start(f32[1,256]{1,0:T(1,128)S(1)} %get-tuple-element.112) | copy-start | bytes 3076
  123.0 14.6 %copy-start.25 = (f32[9,256]{1,0:T(8,128)S(1)}, f32[9,256]{1,0:T(8,128)}, u32[]{:S(2)}) copy-start(f32[9,256]{1,0:T(8,128)} %copy-done.24) | copy-start | bytes 27652
  123.0 165.9 %all-reduce.17.cloned.1.call-start = ((), (), s32[]{:S(2)}) async-start(), calls=%async_computation.1 | async-start | bytes 4718592 | tf_op jit(solution)/shard_map/psum | solution.py:88
  126.9 14.5 %copy-start.32 = (bf16[6,6,256]{2,1,0:T(8,128)(2,1)S(1)}, bf16[6,6,256]{2,1,0:T(8,128)(2,1)}, u32[]{:S(2)}) copy-start(bf16[6,6,256]{2,1,0:T(8,128)(2,1)} %get-tuple-element.70) | copy-start | bytes 55300
  126.9 14.5 %copy-start.31 = (bf16[6,6,256]{2,1,0:T(8,128)(2,1)S(1)}, bf16[6,6,256]{2,1,0:T(8,128)(2,1)}, u32[]{:S(2)}) copy-start(bf16[6,6,256]{2,1,0:T(8,128)(2,1)} %get-tuple-element.71) | copy-start | bytes 55300
  127.0 15.2 %copy-start.30 = (bf16[6,6,256]{2,1,0:T(8,128)(2,1)S(1)}, bf16[6,6,256]{2,1,0:T(8,128)(2,1)}, u32[]{:S(2)}) copy-start(bf16[6,6,256]{2,1,0:T(8,128)(2,1)} %get-tuple-element.72) | copy-start | bytes 55300
  (97 other events, 255.4 us)
Sparse Core Ops, SparseCore 0:
  123.2 53.5 all-reduce.14
  180.3 108.6 all-reduce.16
where the time goes:
time: 301 us; the launch traced here: 299 us
  waiting for transfers between devices  127 us (42%)
  blocking collectives  54.4 us (18%)
  other arithmetic  41.2 us (14%)
  matrix products  34 us (11%)
  local copies, waits for them, and re-layouts  24.6 us (8%)
  between operations  18.1 us (6%)
    psum x1, waiting for transfers between devices, combine_grads(): result = lax.psum(within, 'wide')  106 us
    psum x2, blocking collectives, combine_stats(): result = lax.psum(within, 'wide')  39.7 us
    psum x1, waiting for transfers between devices, combine_grads(): within = lax.psum(values, 'group')  20.6 us
    psum x2, blocking collectives, combine_stats(): within = lax.psum(values, 'group')  14.6 us
    dot_general x36, matrix products, input_grad_rows(): lax.dot_general(window.reshape(row_count * extent, -1), conv_weight[tap_r...  14.1 us
    reshape x24, local copies, waits for them, and re-layouts, input_grad_rows(): window.reshape(row_count * extent, -1)  11.1 us
    dot_general x36, matrix products, conv_rows(): jnp.dot(window.reshape(row_count * extent, -1), conv_weight[tap_row, tap_...  10.4 us
    dot_general x36, matrix products, weight_grad_rows(): lax.dot_general(window.reshape(row_count * extent, -1), flat_back, (((0,)...  9.51 us
  transfers between devices with their start and end apart: 2, of which 2 were waited for; matrix products, arithmetic and copies ran while one was open for 12% of the time, Pallas kernels for 0%

commit v1 on v0

--- a/solution.py
+++ b/solution.py
@@ -1,9 +1,18 @@
+import functools
 import jax
 import jax.numpy as jnp
 from jax import lax
 from jax.sharding import PartitionSpec as P
 
 EPSILON = 1e-05
+
+
+def recast_the_digits(own_rows, along_axis):
+    side_arr = jnp.sum(jax.lax.all_gather(own_rows, along_axis), axis=0)
+    return side_arr
+
+
+view_columns_now = functools.partial(recast_the_digits, along_axis="group")
 
 
 def level_mask(heights, widths, stride, extent):
@@ -84,7 +93,7 @@
 
 
 def combine_grads(values):
-    within = lax.psum(values, "group")
+    within = view_columns_now(values)
     result = lax.psum(within, "wide")
     return result
 

time: 301 us -> 311 us (1.033)
  waiting for transfers between devices: 127 us -> 150 us
  local copies, waits for them, and re-layouts: 24.6 us -> 12.8 us
  matrix products: 34 us -> 28.4 us
  other arithmetic: 41.2 us -> 45.6 us
    all_gather x0 -> x1, waiting for transfers between devices: none -> 47.6 us  [recast_the_digits(): side_arr = jnp.sum(jax.lax.all_gather(own_rows, along_axis), axis=0)]
    psum x1 -> x0, waiting for transfers between devices: 20.6 us -> none  [combine_grads(): within = lax.psum(values, 'group')]
    reshape x24, local copies, waits for them, and re-layouts: 11.1 us -> 0.41 us  [input_grad_rows(): window.reshape(row_count * extent, -1)]
    reduce_sum x0 -> x1, other arithmetic: none -> 6.04 us  [recast_the_digits(): side_arr = jnp.sum(jax.lax.all_gather(own_rows, along_axis), axis=0)]
    dot_general x36, matrix products: 14.1 us -> 8.52 us  [input_grad_rows(): lax.dot_general(window.reshape(row_count * extent, -1), conv_weight[tap_r...]
    psum x1, waiting for transfers between devices: 106 us -> 102 us  [combine_grads(): result = lax.psum(within, 'wide')]
  transfers between devices with their start and end apart: 2 -> 2, of which waited for: 2 -> 2; matrix products, arithmetic and copies ran while one was open for 12% -> 6% of each run, Pallas kernels for 0% -> 0%
where the time goes in v1:
time: 311 us; the launch traced here: 310 us
  waiting for transfers between devices  150 us (48%)
  blocking collectives  54.4 us (17%)
  other arithmetic  45.6 us (15%)
  matrix products  28.4 us (9%)
  between operations  18.1 us (6%)
  local copies, waits for them, and re-layouts  12.8 us (4%)
    psum x1, waiting for transfers between devices, combine_grads(): result = lax.psum(within, 'wide')  102 us
    all_gather x1, waiting for transfers between devices, recast_the_digits(): side_arr = jnp.sum(jax.lax.all_gather(own_rows, along_axis), axis=0)  47.6 us
    psum x2, blocking collectives, combine_stats(): result = lax.psum(within, 'wide')  39.7 us
    psum x2, blocking collectives, combine_stats(): within = lax.psum(values, 'group')  14.8 us
    dot_general x36, matrix products, conv_rows(): jnp.dot(window.reshape(row_count * extent, -1), conv_weight[tap_row, tap_...  10.4 us
    dot_general x36, matrix products, weight_grad_rows(): lax.dot_general(window.reshape(row_count * extent, -1), flat_back, (((0,)...  9.51 us
    dot_general x36, matrix products, input_grad_rows(): lax.dot_general(window.reshape(row_count * extent, -1), conv_weight[tap_r...  8.52 us
  transfers between devices with their start and end apart: 2, of which 2 were waited for; matrix products, arithmetic and copies ran while one was open for 6% of the time, Pallas kernels for 0%

profile of v1, /device:TPU:0, one launch (start us, length us, event | category | flops | bytes accessed | tf_op | source)
XLA Modules:
  0.0 309.5 jit_solution(1283323995085464418)
XLA Ops:
  10.0 0.7 fusion.281
  11.4 0.8 bitcast_multiply_fusion.8
  12.2 0.8 broadcast_multiply_fusion.4
  13.7 0.7 fusion.257
  15.1 0.8 bitcast_multiply_fusion.6
  15.9 0.8 broadcast_multiply_fusion.3
  17.3 1.0 fusion.131
  18.3 1.1 convolution_add_fusion.63
  19.4 1.1 convolution_add_fusion.62
  21.8 0.7 multiply_reduce_fusion.6
  26.4 0.7 multiply_reduce_fusion.4
  31.0 0.7 reshape.1152
  35.5 2.4 pad_maximum_fusion.4
  38.0 8.8 %all-reduce.11 = (f32[4,256]{1,0:T(4,128)S(1)}, f32[4]{0:T(128)S(1)}, f32[4,256]{1,0:T(4,128)S(1)}) all-reduce(f32[4,256]{1,0:T(4,128)S(1)} %pad_maximum_fusion.1, f32[4]{0:T(128)S(1)} %pad_maximum_fusion.4, f32[4,256]{1,0:T(4,128)S(1)} %pad_maximum_fusion), channel_id=1, replica_groups=mesh['wide'=8,'group'=4] {'group'}, use_global_device_ids=true, to_apply=%region_16.17 | all-reduce | flops 2052 | bytes 16416 | tf_op jit(solution)/shard_map/psum | solution.py:90
  46.7 22.1 %all-reduce.9 = (f32[4,256]{1,0:T(4,128)S(1)}, f32[4]{0:T(128)S(1)}, f32[4,256]{1,0:T(4,128)S(1)}) all-reduce(f32[4,256]{1,0:T(4,128)S(1)} %get-tuple-element.34, f32[4]{0:T(128)S(1)} %get-tuple-element.35, f32[4,256]{1,0:T(4,128)S(1)} %get-tuple-element.36), channel_id=1, replica_groups=mesh['wide'=8,'group'=4] {'wide'}, use_global_device_ids=true, to_apply=%region_17.18 | all-reduce | flops 2052 | bytes 16416 | tf_op jit(solution)/shard_map/psum | solution.py:91
  69.5 2.5 slice_divide_fusion.8
  72.0 2.5 slice_divide_fusion.9
  78.4 6.0 %all-reduce.10 = (f32[4,256]{1,0:T(4,128)S(1)}, f32[4,256]{1,0:T(4,128)S(1)}) all-reduce(f32[4,256]{1,0:T(4,128)S(1)} %pad_maximum_fusion.3, f32[4,256]{1,0:T(4,128)S(1)} %pad_maximum_fusion.2), channel_id=1, replica_groups=mesh['wide'=8,'group'=4] {'group'}, use_global_device_ids=true, to_apply=%region_28.29 | all-reduce | flops 2048 | bytes 16384 | tf_op jit(solution)/shard_map/psum | solution.py:90
  84.4 17.6 %all-reduce.8 = (f32[4,256]{1,0:T(4,128)S(1)}, f32[4,256]{1,0:T(4,128)S(1)}) all-reduce(f32[4,256]{1,0:T(4,128)S(1)} %get-tuple-element.32, f32[4,256]{1,0:T(4,128)S(1)} %get-tuple-element.33), channel_id=1, replica_groups=mesh['wide'=8,'group'=4] {'wide'}, use_global_device_ids=true, to_apply=%region_29.30 | all-reduce | flops 2048 | bytes 16384 | tf_op jit(solution)/shard_map/psum | solution.py:91
  102.0 2.5 slice_divide_fusion
  104.5 2.5 slice_divide_fusion.1
  107.1 1.1 multiply_convert_fusion.2
  120.2 2.1 add_add_fusion
  129.1 1.2 convolution_add_fusion.20
  131.1 0.7 reshape.1176
  131.9 1.2 pad_slice_fusion
  136.9 47.6 %all-gather.2.cloned.1.call-done = f32[4,3,3,256,256]{4,3,2,1,0:T(8,128)} async-done(((f32[1,3,3,256,256]{4,3,2,1,0:T(8,128)}), f32[4,3,3,256,256]{4,3,2,1,0:T(8,128)}) %all-gather.2.cloned.1.call-update) | async-done | bytes 9437200 | tf_op jit(solution)/shard_map/all_gather | solution.py:11
  184.6 6.0 %reduce_sum.209 = f32[3,3,256,256]{3,2,1,0:T(8,128)} reduce(f32[4,3,3,256,256]{4,3,2,1,0:T(8,128)} %all-gather.2.cloned.1.call-done, f32[]{:T(128)} %constant.111.clone.1), dimensions={0}, to_apply=%region_30.31 | reduce | flops 1769472 | bytes 11796484 | tf_op jit(solution)/shard_map/reduce_sum | solution.py:11
  191.2 1.8 multiply_convert_fusion.6
  196.2 1.1 multiply_convert_fusion.1
  197.2 102.2 %all-reduce.14.cloned.1.call-done = f32[3,3,256,256]{3,2,1,0:T(8,128)} async-done(((f32[3,3,256,256]{3,2,1,0:T(8,128)}), f32[3,3,256,256]{3,2,1,0:T(8,128)}) %all-reduce.14.cloned.1.call-update) | async-done | bytes 2359312 | tf_op jit(solution)/shard_map/psum | solution.py:97
  299.4 3.3 %broadcast_multiply_fusion = f32[3,3,256,256]{3,2,1,0:T(8,128)} fusion(f32[3,3,256,256]{3,2,1,0:T(8,128)} %all-reduce.14.cloned.1.call-done), kind=kLoop, calls=%fused_computation.17 | loop fusion | flops 589824 | bytes 4718592 | tf_op jit(solution)/shard_map/div | solution.py:200
  (497 shorter events, 46.3 us)
Async XLA Ops:
  7.2 13.3 %copy-start = (bf16[3,3,256,256]{3,2,1,0:T(8,128)(2,1)S(1)}, bf16[3,3,256,256]{3,2,1,0:T(8,128)(2,1)}, u32[]{:S(2)}) copy-start(bf16[3,3,256,256]{3,2,1,0:T(8,128)(2,1)} %param.21) | copy-start | bytes 3538948
  7.2 16.6 %copy-start.9 = (bf16[1,12,12,256]{3,2,1,0:T(8,128)(2,1)S(1)}, bf16[1,12,12,256]{3,2,1,0:T(8,128)(2,1)}, u32[]{:S(2)}) copy-start(bf16[1,12,12,256]{3,2,1,0:T(8,128)(2,1)} %param.14) | copy-start | bytes 221188
  7.2 177.4 %all-gather.2.cloned.1.call-start = ((), (), s32[]{:S(2)}) async-start(), calls=%async_computation | async-start | bytes 11796480 | tf_op jit(solution)/shard_map/all_gather | solution.py:11
  32.2 44.7 %copy-start.39 = (f32[1,256]{1,0:T(1,128)}, f32[1,256]{1,0:T(1,128)S(1)}, u32[]{:S(2)}) copy-start(f32[1,256]{1,0:T(1,128)S(1)} %get-tuple-element.118) | copy-start | bytes 3076
  32.2 45.1 %copy-start.60 = (f32[1,256]{1,0:T(1,128)}, f32[1,256]{1,0:T(1,128)S(1)}, u32[]{:S(2)}) copy-start(f32[1,256]{1,0:T(1,128)S(1)} %get-tuple-element.117) | copy-start | bytes 3076
  32.2 45.3 %copy-start.62 = (f32[1,256]{1,0:T(1,128)}, f32[1,256]{1,0:T(1,128)S(1)}, u32[]{:S(2)}) copy-start(f32[1,256]{1,0:T(1,128)S(1)} %get-tuple-element.119) | copy-start | bytes 3076
  32.2 45.4 %copy-start.92 = (f32[1,256]{1,0:T(1,128)}, f32[1,256]{1,0:T(1,128)S(1)}, u32[]{:S(2)}) copy-start(f32[1,256]{1,0:T(1,128)S(1)} %get-tuple-element.116) | copy-start | bytes 3076
  32.2 44.6 %copy-start.50 = (f32[1,256]{1,0:T(1,128)}, f32[1,256]{1,0:T(1,128)S(1)}, u32[]{:S(2)}) copy-start(f32[1,256]{1,0:T(1,128)S(1)} %get-tuple-element.130) | copy-start | bytes 3076
  32.2 45.0 %copy-start.78 = (f32[1,256]{1,0:T(1,128)}, f32[1,256]{1,0:T(1,128)S(1)}, u32[]{:S(2)}) copy-start(f32[1,256]{1,0:T(1,128)S(1)} %get-tuple-element.129) | copy-start | bytes 3076
  32.3 45.2 %copy-start.81 = (f32[1,256]{1,0:T(1,128)}, f32[1,256]{1,0:T(1,128)S(1)}, u32[]{:S(2)}) copy-start(f32[1,256]{1,0:T(1,128)S(1)} %get-tuple-element.131) | copy-start | bytes 3076
  32.3 45.3 %copy-start.95 = (f32[1,256]{1,0:T(1,128)}, f32[1,256]{1,0:T(1,128)S(1)}, u32[]{:S(2)}) copy-start(f32[1,256]{1,0:T(1,128)S(1)} %get-tuple-element.128) | copy-start | bytes 3076
  34.5 42.3 %copy-start.1 = (bf16[1,24,24,256]{3,2,1,0:T(8,128)(2,1)S(1)}, bf16[1,24,24,256]{3,2,1,0:T(8,128)(2,1)}, u32[]{:S(2)}) copy-start(bf16[1,24,24,256]{3,2,1,0:T(8,128)(2,1)} %param.17) | copy-start | bytes 884740
  34.5 42.3 %copy-start.16 = (f32[24,24]{1,0:T(8,128)S(1)}, f32[24,24]{1,0:T(8,128)}, u32[]{:S(2)}) copy-start(f32[24,24]{1,0:T(8,128)} %get-tuple-element.150) | copy-start | bytes 6916
  35.2 42.1 %copy-start.7 = (bf16[1,12,12,256]{3,2,1,0:T(8,128)(2,1)S(1)}, bf16[1,12,12,256]{3,2,1,0:T(8,128)(2,1)}, u32[]{:S(2)}) copy-start(bf16[1,12,12,256]{3,2,1,0:T(8,128)(2,1)} %param.18) | copy-start | bytes 221188
  35.2 42.3 %copy-start.14 = (bf16[1,6,6,256]{3,2,1,0:T(8,128)(2,1)S(1)}, bf16[1,6,6,256]{3,2,1,0:T(8,128)(2,1)}, u32[]{:S(2)}) copy-start(bf16[1,6,6,256]{3,2,1,0:T(8,128)(2,1)} %param.19) | copy-start | bytes 55300
  35.2 42.3 %copy-start.29 = (f32[6,6]{1,0:T(8,128)S(1)}, f32[6,6]{1,0:T(8,128)}, u32[]{:S(2)}) copy-start(f32[6,6]{1,0:T(8,128)} %get-tuple-element.146) | copy-start | bytes 436
  35.2 42.5 %copy-start.23 = (f32[3,3,256]{2,1,0:T(4,128)S(1)}, f32[3,3,256]{2,1,0:T(4,128)}, u32[]{:S(2)}) copy-start(f32[3,3,256]{2,1,0:T(4,128)} %reshape.1158) | copy-start | bytes 27652
  35.2 42.5 %copy-start.43 = (f32[3,3]{1,0:T(4,128)S(1)}, f32[3,3]{1,0:T(4,128)}, u32[]{:S(2)}) copy-start(f32[3,3]{1,0:T(4,128)} %get-tuple-element.144) | copy-start | bytes 112
  35.2 42.5 %copy-start.68 = (bf16[1,3,3,256]{3,2,1,0:T(4,128)(2,1)S(1)}, bf16[1,3,3,256]{3,2,1,0:T(4,128)(2,1)}, u32[]{:S(2)}) copy-start(bf16[1,3,3,256]{3,2,1,0:T(4,128)(2,1)} %param.20) | copy-start | bytes 13828
  74.5 32.5 %copy-start.36 = (f32[1,256]{1,0:T(1,128)}, f32[1,256]{1,0:T(1,128)S(1)}, u32[]{:S(2)}) copy-start(f32[1,256]{1,0:T(1,128)S(1)} %get-tuple-element.123) | copy-start | bytes 3076
  74.5 32.5 %copy-start.54 = (f32[1,256]{1,0:T(1,128)}, f32[1,256]{1,0:T(1,128)S(1)}, u32[]{:S(2)}) copy-start(f32[1,256]{1,0:T(1,128)S(1)} %get-tuple-element.122) | copy-start | bytes 3076
  74.6 32.5 %copy-start.57 = (f32[1,256]{1,0:T(1,128)}, f32[1,256]{1,0:T(1,128)S(1)}, u32[]{:S(2)}) copy-start(f32[1,256]{1,0:T(1,128)S(1)} %get-tuple-element.121) | copy-start | bytes 3076
  74.6 32.5 %copy-start.65 = (f32[1,256]{1,0:T(1,128)}, f32[1,256]{1,0:T(1,128)S(1)}, u32[]{:S(2)}) copy-start(f32[1,256]{1,0:T(1,128)S(1)} %get-tuple-element.120) | copy-start | bytes 3076
  75.2 31.9 %copy-start.75 = (f32[256]{0:T(256)}, f32[256]{0:T(256)S(1)}, u32[]{:S(2)}) copy-start(f32[256]{0:T(256)S(1)} %get-tuple-element.137) | copy-start | bytes 3076
  75.7 31.4 %copy-start.85 = (f32[256]{0:T(256)}, f32[256]{0:T(256)S(1)}, u32[]{:S(2)}) copy-start(f32[256]{0:T(256)S(1)} %get-tuple-element.135) | copy-start | bytes 3076
  76.3 30.8 %copy-start.72 = (f32[256]{0:T(256)}, f32[256]{0:T(256)S(1)}, u32[]{:S(2)}) copy-start(f32[256]{0:T(256)S(1)} %get-tuple-element.139) | copy-start | bytes 3076
  76.9 30.3 %copy-start.46 = (f32[256]{0:T(256)}, f32[256]{0:T(256)S(1)}, u32[]{:S(2)}) copy-start(f32[256]{0:T(256)S(1)} %get-tuple-element.141) | copy-start | bytes 3076
  104.5 11.5 %copy-start.120 = (f32[1,256]{1,0:T(1,128)}, f32[1,256]{1,0:T(1,128)S(1)}, u32[]{:S(2)}) copy-start(f32[1,256]{1,0:T(1,128)S(1)} %get-tuple-element.110) | copy-start | bytes 3076
  104.5 14.0 %copy-start.107 = (f32[1,256]{1,0:T(1,128)}, f32[1,256]{1,0:T(1,128)S(1)}, u32[]{:S(2)}) copy-start(f32[1,256]{1,0:T(1,128)S(1)} %get-tuple-element.112) | copy-start | bytes 3076
  107.0 9.0 %copy-start.122 = (f32[1,256]{1,0:T(1,128)}, f32[1,256]{1,0:T(1,128)S(1)}, u32[]{:S(2)}) copy-start(f32[1,256]{1,0:T(1,128)S(1)} %get-tuple-element.106) | copy-start | bytes 3076
  107.0 11.4 %copy-start.109 = (f32[1,256]{1,0:T(1,128)}, f32[1,256]{1,0:T(1,128)S(1)}, u32[]{:S(2)}) copy-start(f32[1,256]{1,0:T(1,128)S(1)} %get-tuple-element.108) | copy-start | bytes 3076
  122.4 177.1 %all-reduce.14.cloned.1.call-start = ((), (), s32[]{:S(2)}) async-start(), calls=%async_computation.1 | async-start | bytes 4718592 | tf_op jit(solution)/shard_map/psum | solution.py:97
  (99 other events, 221.3 us)
Sparse Core Ops, SparseCore 0:
  122.4 62.1 all-gather.1
  190.8 108.5 all-reduce.13
